TPU v7x, 32 devices: a whole 2x2x4 slice. The times are simulated.
32 devices in a mesh: seq: 8 (over z, y), head: 4 (over x, core).
Axes of the slice: x: 2, y: 2, z: 4, core: 2. Of those that a mesh axis runs over, the one named last changes fastest.
Arguments:
- query_rows: bfloat16 [8192, 4096], P('seq', 'head'), may hold values from -6 to 6
- key_rows: bfloat16 [8192, 4096], P('seq', 'head'), may hold values from -6 to 6
- value_rows: bfloat16 [8192, 4096], P('seq', 'head'), may hold values from -15 to 15
- block_picks: int32 [16, 32, 4], P('seq', 'head'), may hold values from -1 to 15, as said below
- out_weight: bfloat16 [4096, 4096], P(None, 'head'), may hold values from -0.09375 to 0.09375
Outputs:
- mixed: bfloat16 [8192, 4096], P('seq', 'head')
Inputs may be any that keep to these rules, and one draw needn't show every extreme that they name: `block_picks`: every entry that is not -1 names a block held by a lower index of seq than block b. Repeated entries of one row count once. Over the query blocks of one index of seq and the heads of one index of head, at most 2 entries name blocks of any one other index of seq, and every index of seq from 1 on has exactly 2 entries naming blocks of index 0.
All inputs are finite; a program needn't handle non-finite values.
Results may differ from a plain program's by a relative error of at most 0.0059.
Values may be sent and summed in bfloat16 or wider, within the bound.
A program may use at most 192 MiB of HBM per device.

v0:
```python
import jax
import jax.numpy as jnp
from jax import lax
from jax.sharding import PartitionSpec as P

CAP = 2


def tile_partial(query_tile, key_tile, value_tile, causal_mask):
    score_scale = query_tile.shape[-1] ** (-0.5)
    scores = (
        jnp.einsum("nqd,nkd->nqk", query_tile, key_tile, preferred_element_type=jnp.float32)
        * score_scale
    )
    if causal_mask is not None:
        scores = jnp.where(causal_mask, scores, -jnp.inf)
    maxima = jnp.max(scores, axis=-1)
    shifted = jnp.exp(scores - maxima[..., None])
    totals = jnp.sum(shifted, axis=-1)
    weights = shifted.astype(jnp.bfloat16)
    partial_out = jnp.einsum(
        "nqk,nkd->nqd", weights, value_tile, preferred_element_type=jnp.float32
    )
    return (partial_out.astype(jnp.bfloat16), maxima, totals)


def grouped_partial(query_tile, key_tile, value_tile):
    tile_count = query_tile.shape[0]
    groups = 1
    while tile_count % (groups * 2) == 0 and tile_count // groups > 16:
        groups = groups * 2
    if groups == 1:
        return tile_partial(query_tile, key_tile, value_tile, None)

    def one_group(operands):
        return tile_partial(operands[0], operands[1], operands[2], None)

    reshaped = tuple(
        (
            operand.reshape((groups, tile_count // groups) + operand.shape[1:])
            for operand in (query_tile, key_tile, value_tile)
        )
    )
    results = lax.map(one_group, reshaped)
    return tuple(
        (result_array.reshape((tile_count,) + result_array.shape[2:]) for result_array in results)
    )


def plan_slots(picks_local, per_device, seq_count, capacity):
    blocks_here, heads_here, pick_count = picks_local.shape
    usable_cols = []
    for column in range(pick_count):
        entries = picks_local[:, :, column]
        is_fresh = entries >= 0
        for earlier in range(column):
            is_fresh = is_fresh & (entries != picks_local[:, :, earlier])
        usable_cols.append(is_fresh)
    usable = jnp.stack(usable_cols, 2).reshape(-1)
    flat_picks = picks_local.reshape(-1)
    owner_dev = jnp.where(usable, flat_picks // per_device, -1)
    onehot = (owner_dev[:, None] == jnp.arange(seq_count, dtype=jnp.int32)[None, :]).astype(
        jnp.int32
    )
    before = jnp.cumsum(onehot, axis=0) - onehot
    bucket_rank = jnp.sum(before * onehot, axis=1)
    slot_index = jnp.where(usable, owner_dev * capacity + bucket_rank, -1)
    entry_ids = jnp.arange(flat_picks.shape[0], dtype=jnp.int32)
    head_of = entry_ids // pick_count % heads_here
    tile_code = jnp.maximum(flat_picks, 0) % per_device * heads_here + head_of
    matches = slot_index[:, None] == jnp.arange(seq_count * capacity, dtype=jnp.int32)[None, :]
    request_table = jnp.sum(jnp.where(matches, tile_code[:, None] + 1, 0), axis=0) - 1
    sender = jnp.sum(jnp.where(matches, entry_ids[:, None], 0), axis=0)
    return (usable, jnp.maximum(slot_index, 0), request_table.reshape(seq_count, capacity), sender)


def body(query_rows, key_rows, value_rows, block_picks, out_weight):
    seq_count = lax.axis_size("seq")
    capacity = CAP
    tok_rows, feature_width = query_rows.shape
    blocks_here, heads_here, pick_count = block_picks.shape
    block_rows = tok_rows // blocks_here
    head_width = feature_width // heads_here
    pair_count = blocks_here * heads_here

    def by_head(rows_in):
        shaped = rows_in.reshape(blocks_here, block_rows, heads_here, head_width)
        return jnp.transpose(shaped, (0, 2, 1, 3)).reshape(pair_count, block_rows, head_width)

    query_tiles = by_head(query_rows)
    key_tiles = by_head(key_rows)
    value_tiles = by_head(value_rows)
    positions = jnp.arange(block_rows)
    causal_mask = (positions[:, None] >= positions[None, :])[None]
    own_out, own_max, own_total = tile_partial(query_tiles, key_tiles, value_tiles, causal_mask)
    usable, slot_index, request_table, sender = plan_slots(
        block_picks, blocks_here, seq_count, capacity
    )
    incoming = lax.all_to_all(request_table, "seq", split_axis=0, concat_axis=0, tiled=True)
    wanted = jnp.maximum(incoming, 0).reshape(-1)
    asking = jnp.broadcast_to(
        query_tiles[:, None], (pair_count, pick_count, block_rows, head_width)
    )
    asking = asking.reshape(pair_count * pick_count, block_rows, head_width)
    outgoing = asking[sender].reshape(seq_count, capacity, block_rows, head_width)
    arrived = lax.all_to_all(outgoing, "seq", split_axis=0, concat_axis=0, tiled=True)
    arrived = arrived.reshape(seq_count * capacity, block_rows, head_width)
    served_out, served_max, served_total = grouped_partial(
        arrived, key_tiles[wanted], value_tiles[wanted]
    )
    back_out = lax.all_to_all(
        served_out.reshape(seq_count, capacity, block_rows, head_width),
        "seq",
        split_axis=0,
        concat_axis=0,
        tiled=True,
    )
    back_max, back_total = (
        lax.all_to_all(
            served_max.reshape(seq_count, capacity, block_rows),
            "seq",
            split_axis=0,
            concat_axis=0,
            tiled=True,
        ),
        lax.all_to_all(
            served_total.reshape(seq_count, capacity, block_rows),
            "seq",
            split_axis=0,
            concat_axis=0,
            tiled=True,
        ),
    )
    far_out = back_out.reshape(seq_count * capacity, block_rows, head_width)[slot_index]
    far_max = back_max.reshape(seq_count * capacity, block_rows)[slot_index]
    far_total = back_total.reshape(seq_count * capacity, block_rows)[slot_index]
    all_out = jnp.concatenate(
        [own_out[:, None], far_out.reshape(pair_count, pick_count, block_rows, head_width)], 1
    )
    all_max = jnp.concatenate(
        [own_max[:, None], far_max.reshape(pair_count, pick_count, block_rows)], 1
    )
    all_total = jnp.concatenate(
        [own_total[:, None], far_total.reshape(pair_count, pick_count, block_rows)], 1
    )
    all_usable = jnp.concatenate(
        [jnp.ones((pair_count, 1), dtype=jnp.bool_), usable.reshape(pair_count, pick_count)], 1
    )
    keep = all_usable[:, :, None]
    largest = jnp.max(jnp.where(keep, all_max, -jnp.inf), axis=1)
    factor = jnp.where(keep, jnp.exp(all_max - largest[:, None]), 0.0)
    numer = jnp.sum(factor[..., None] * all_out.astype(jnp.float32), axis=1)
    denom = jnp.sum(factor * all_total, axis=1)
    combined = (numer / denom[..., None]).astype(jnp.bfloat16)
    combined = combined.reshape(blocks_here, heads_here, block_rows, head_width)
    attended = jnp.transpose(combined, (0, 2, 1, 3)).reshape(tok_rows, feature_width)
    mixed = jnp.dot(
        lax.all_gather(attended, "head", axis=1, tiled=True),
        out_weight,
        preferred_element_type=jnp.float32,
    )
    return mixed.astype(jnp.bfloat16)


def solution(mesh):
    return jax.shard_map(
        body,
        mesh=mesh,
        in_specs=(
            P("seq", "head"),
            P("seq", "head"),
            P("seq", "head"),
            P("seq", "head", None),
            P(None, "head"),
        ),
        out_specs=P("seq", "head"),
        check_vma=False,
    )
```

profile of v0, /device:TPU:17, one launch (start us, length us, event | category | flops | bytes accessed | tf_op | source)
XLA Modules:
  0.0 279.9 jit_solution(9715517587896974524)
XLA Ops:
  6.5 0.9 fusion.44
  7.4 0.8 copy.61
  8.2 0.1 copy.60
  8.3 0.1 reshape.327
  8.4 0.1 reshape.328
  8.5 0.1 fusion.29
  8.6 0.1 reduce_window_sum.11
  8.7 0.2 select_reduce_fusion.1
  8.9 0.1 select_reduce_fusion.3
  9.0 0.7 sub.52
  9.7 5.6 %all-to-all-start.1 = ((s32[8,1,2]{2,1,0:T(1,128)}), s32[8,1,2]{2,1,0:T(1,128)S(1)}, u32[]{:S(2)}, u32[]{:S(2)}) async-start(s32[8,1,2]{2,1,0:T(1,128)} %bitcast.10), calls=%async_computation.1 | async-start | bytes 8192 | tf_op jit(solution)/shard_map/all_to_all | solution.py:99
  15.3 2.2 copy.74
  17.5 0.1 bitcast_bitcast_fusion.2
  17.7 0.4 copy.58
  18.1 5.2 %broadcast_in_dim.87 = bf16[16,4,512,128]{3,2,1,0:T(8,128)(2,1)} broadcast(bf16[16,512,128]{2,1,0:T(8,128)(2,1)S(1)} %bitcast.69), dimensions={0,2,3} | broadcast | bytes 10485760 | tf_op jit(solution)/shard_map/broadcast_in_dim | solution.py:101
  23.3 5.7 %gather_fusion = bf16[16,512,128]{2,1,0:T(8,128)(2,1)} fusion(bf16[64,512,128]{2,1,0:T(8,128)(2,1)} %bitcast.74, s32[1024]{0:T(1024)S(1)} %pad_clamp_fusion.2), kind=kCustom, calls=%fused_computation | custom fusion | bytes 4194368 | tf_op jit(solution)/shard_map/gather | solution.py:105
  29.0 0.0 all-to-all-done.1
  29.0 5.4 %all-to-all-start = ((bf16[8,2,512,128]{3,2,1,0:T(8,128)(2,1)}), bf16[8,2,512,128]{3,2,1,0:T(8,128)(2,1)}, u32[]{:S(2)}, u32[]{:S(2)}) async-start(bf16[8,2,512,128]{3,2,1,0:T(8,128)(2,1)} %bitcast.8), calls=%async_computation | async-start | bytes 4194304 | tf_op jit(solution)/shard_map/all_to_all | solution.py:106
  34.5 0.1 reshape.333
  34.6 0.1 reshape.334
  34.7 0.1 stack.18
  34.8 0.1 stack.17
  34.8 0.1 stack.19
  34.9 0.1 stack.20
  35.0 0.6 copy.75
  35.6 0.0 copy-start.4
  35.6 0.1 bitcast_bitcast_fusion.1
  35.8 0.4 copy.59
  36.2 1.2 copy-done.4
  37.4 0.6 copy.76
  38.1 0.1 iota_compare_fusion
  38.1 1.5 bitcast_bitcast_fusion
  39.6 0.1 reshape.354
  39.7 2.2 gather_fusion.1
  41.9 36.5 %all-to-all-done = bf16[8,2,512,128]{3,2,1,0:T(8,128)(2,1)} async-done(((bf16[8,2,512,128]{3,2,1,0:T(8,128)(2,1)}), bf16[8,2,512,128]{3,2,1,0:T(8,128)(2,1)}, u32[]{:S(2)}, u32[]{:S(2)}) %all-to-all-start) | async-done | bytes 2097184 | tf_op jit(solution)/shard_map/all_to_all | solution.py:106
  78.4 10.3 %multiply_reduce_fusion.1 = (f32[16,512]{1,0:T(8,128)S(1)}, f32[16,512,512]{1,2,0:T(8,128)}) fusion(bf16[16,512,128]{2,1,0:T(8,128)(2,1)} %bitcast.9, bf16[16,512,128]{2,1,0:T(8,128)(2,1)} %gather_fusion.1), kind=kOutput, calls=%fused_computation.11 | convolution fusion | flops 1082122240 | bytes 21004288 | tf_op jit(solution)/shard_map/nqd,nkd->nqk/dot_general | solution.py:12
  88.6 8.7 %fusion.2 = f32[16,512]{1,0:T(8,128)S(1)} fusion(f32[16,512,512]{1,2,0:T(8,128)} %get-tuple-element.24, f32[16,512]{1,0:T(8,128)S(1)} %get-tuple-element.23), kind=kLoop, calls=%fused_computation.13 | loop fusion | flops 12574720 | bytes 16842752 | tf_op jit(solution)/shard_map/reduce_sum | solution.py:19
  97.3 0.6 reshape.340
  98.0 8.3 %all-to-all-start.4 = ((f32[8,2,512]{2,1,0:T(2,128)}), f32[8,2,512]{2,1,0:T(2,128)S(1)}, u32[]{:S(2)}, u32[]{:S(2)}) async-start(f32[8,2,512]{2,1,0:T(2,128)} %reshape.340), calls=%async_computation.4 | async-start | bytes 65536 | tf_op jit(solution)/shard_map/all_to_all | solution.py:126
  106.3 0.1 copy.73
  106.4 1.7 copy.66
  108.1 2.5 gather_fusion.3
  110.6 0.6 reshape.331
  111.2 0.0 all-to-all-done.4
  111.2 5.4 %all-to-all-start.2 = ((f32[8,2,512]{2,1,0:T(2,128)}), f32[8,2,512]{2,1,0:T(2,128)S(1)}, u32[]{:S(2)}, u32[]{:S(2)}) async-start(f32[8,2,512]{2,1,0:T(2,128)} %reshape.331), calls=%async_computation.2 | async-start | bytes 65536 | tf_op jit(solution)/shard_map/all_to_all | solution.py:119
  116.7 10.7 %fusion.17 = bf16[16,512,128]{2,1,0:T(8,128)(2,1)} fusion(bf16[16,512,128]{2,1,0:T(8,128)(2,1)S(1)} %gather_fusion.3, f32[16,512,512]{1,2,0:T(8,128)} %get-tuple-element.24, f32[16,512]{1,0:T(8,128)S(1)} %get-tuple-element.23), kind=kOutput, calls=%fused_computation.33 | convolution fusion | flops 1087373312 | bytes 21004288 | tf_op jit(solution)/shard_map/nqk,nkd->nqd/dot_general | solution.py:21
  127.4 0.0 all-to-all-done.2
  127.4 5.4 %all-to-all-start.3 = ((bf16[8,2,512,128]{3,2,1,0:T(8,128)(2,1)}), bf16[8,2,512,128]{3,2,1,0:T(8,128)(2,1)S(1)}, u32[]{:S(2)}, u32[]{:S(2)}) async-start(bf16[8,2,512,128]{3,2,1,0:T(8,128)(2,1)} %bitcast.75), calls=%async_computation.3 | async-start | bytes 4194304 | tf_op jit(solution)/shard_map/all_to_all | solution.py:111
  132.8 10.4 %fusion.1 = (f32[16,512]{1,0:T(8,128)S(1)}, f32[16,512,512]{1,2,0:T(8,128)}) fusion(pred[512,512]{0,1:T(8,128)(4,1)S(1)} %iota_compare_fusion, bf16[16,512,128]{2,1,0:T(8,128)(2,1)} %bitcast.70, bf16[16,512,128]{2,1,0:T(8,128)(2,1)} %bitcast.72), kind=kOutput, calls=%fused_computation.12 | convolution fusion | flops 1086316544 | bytes 21266432 | tf_op jit(solution)/shard_map/nqd,nkd->nqk/dot_general | solution.py:12
  143.3 9.1 %fusion.4 = f32[16,512]{1,0:T(8,128)S(1)} fusion(f32[16,512,512]{1,2,0:T(8,128)} %get-tuple-element.26, f32[16,512]{1,0:T(8,128)S(1)} %get-tuple-element.25, pred[512,512]{0,1:T(8,128)(4,1)S(1)} %iota_compare_fusion), kind=kLoop, calls=%fused_computation.15 | loop fusion | flops 16769024 | bytes 17104896 | tf_op jit(solution)/shard_map/reduce_sum | solution.py:19
  152.5 0.1 concatenate.21.clone
  152.6 12.3 %convert_bitcast_fusion = bf16[16,1,512,128]{3,2,1,0:T(8,128)(2,1)} fusion(bf16[16,512,128]{2,1,0:T(8,128)(2,1)} %bitcast.77, f32[16,512,512]{1,2,0:T(8,128)} %get-tuple-element.26, f32[16,512]{1,0:T(8,128)S(1)} %get-tuple-element.25, pred[512,512]{0,1:T(8,128)(4,1)S(1)} %iota_compare_fusion), kind=kOutput, calls=%fused_computation.30 | convolution fusion | flops 1091567616 | bytes 21266432 | tf_op jit(solution)/shard_map/nqk,nkd->nqd/dot_general | solution.py:21
  164.9 0.7 gather_fusion.2
  165.7 0.7 gather_fusion.5
  166.4 2.1 fusion.26
  168.5 7.8 %all-to-all-done.3 = bf16[8,2,512,128]{3,2,1,0:T(8,128)(2,1)S(1)} async-done(((bf16[8,2,512,128]{3,2,1,0:T(8,128)(2,1)}), bf16[8,2,512,128]{3,2,1,0:T(8,128)(2,1)S(1)}, u32[]{:S(2)}, u32[]{:S(2)}) %all-to-all-start.3) | async-done | bytes 2097184 | tf_op jit(solution)/shard_map/all_to_all | solution.py:111
  176.3 5.3 %gather_fusion.4 = bf16[64,512,128]{2,1,0:T(8,128)(2,1)} fusion(bf16[16,512,128]{2,1,0:T(8,128)(2,1)S(1)} %bitcast.67, s32[1024]{0:T(1024)S(1)} %pad_clamp_fusion), kind=kCustom, calls=%fused_computation.4 | custom fusion | bytes 16777472 | tf_op jit(solution)/shard_map/gather | solution.py:134
  181.6 9.4 %multiply_reduce_fusion = f32[16,512,128]{2,1,0:T(8,128)S(1)} fusion(bf16[16,4,512,128]{3,2,1,0:T(8,128)(2,1)} %bitcast.68, bf16[16,1,512,128]{3,2,1,0:T(8,128)(2,1)} %convert_bitcast_fusion, f32[16,5,512]{2,1,0:T(8,128)S(1)} %get-tuple-element.28), kind=kLoop, calls=%fused_computation.7 | loop fusion | flops 19922944 | bytes 14843904 | tf_op jit(solution)/shard_map/reduce_sum | solution.py:152
  191.0 1.4 fusion.16
  192.4 1.4 copy.70
  193.8 1.9 copy.79
  195.7 0.0 all-gather.2.cloned.1.call-update
  195.8 62.7 %all-gather.2.cloned.1.call-done = bf16[1024,4096]{1,0:T(8,128)(2,1)} async-done(((bf16[1024,1024]{1,0:T(8,128)(2,1)}), bf16[1024,4096]{1,0:T(8,128)(2,1)}) %all-gather.2.cloned.1.call-update) | async-done | bytes 8388624 | tf_op jit(solution)/shard_map/all_gather | solution.py:158
  258.4 14.6 %convolution_convert_fusion = bf16[1024,1024]{1,0:T(8,128)(2,1)} fusion(bf16[1024,4096]{1,0:T(8,128)(2,1)} %all-gather.2.cloned.1.call-done, bf16[4096,1024]{1,0:T(8,128)(2,1)} %param.9), kind=kOutput, calls=%fused_computation.32 | convolution fusion | flops 8590983168 | bytes 18874368 | tf_op jit(solution)/shard_map/dot_general | solution.py:157
  (26 shorter events, 0.3 us)
Async XLA Ops:
  9.7 19.4 %all-to-all-start.1 = ((s32[8,1,2]{2,1,0:T(1,128)}), s32[8,1,2]{2,1,0:T(1,128)S(1)}, u32[]{:S(2)}, u32[]{:S(2)}) async-start(s32[8,1,2]{2,1,0:T(1,128)} %bitcast.10), calls=%async_computation.1 | async-start | bytes 8192 | tf_op jit(solution)/shard_map/all_to_all | solution.py:99
  18.0 5.3 %copy-start = (bf16[2,8,512,128]{3,2,1,0:T(8,128)(2,1)}, bf16[2,8,512,128]{3,2,1,0:T(8,128)(2,1)S(1)}, u32[]{:S(2)}) copy-start(bf16[2,8,512,128]{3,2,1,0:T(8,128)(2,1)S(1)} %copy.58) | copy-start | bytes 6291460
  23.3 11.7 %copy-start.3 = (bf16[1024,1024]{1,0:T(8,128)(2,1)S(1)}, bf16[1024,1024]{1,0:T(8,128)(2,1)}, u32[]{:S(2)}) copy-start(bf16[1024,1024]{1,0:T(8,128)(2,1)} %param.6) | copy-start | bytes 6291460
  29.0 49.3 %all-to-all-start = ((bf16[8,2,512,128]{3,2,1,0:T(8,128)(2,1)}), bf16[8,2,512,128]{3,2,1,0:T(8,128)(2,1)}, u32[]{:S(2)}, u32[]{:S(2)}) async-start(bf16[8,2,512,128]{3,2,1,0:T(8,128)(2,1)} %bitcast.8), calls=%async_computation | async-start | bytes 4194304 | tf_op jit(solution)/shard_map/all_to_all | solution.py:106
  35.6 1.8 copy-start.4
  36.2 3.5 %copy-start.1 = (bf16[2,8,512,128]{3,2,1,0:T(8,128)(2,1)}, bf16[2,8,512,128]{3,2,1,0:T(8,128)(2,1)S(1)}, u32[]{:S(2)}) copy-start(bf16[2,8,512,128]{3,2,1,0:T(8,128)(2,1)S(1)} %copy.59) | copy-start | bytes 6291460
  88.6 17.7 %copy-start.2 = (bf16[2,8,512,128]{3,1,2,0:T(8,128)(2,1)S(1)}, bf16[2,8,512,128]{3,1,2,0:T(8,128)(2,1)}, u32[]{:S(2)}) copy-start(bf16[2,8,512,128]{3,1,2,0:T(8,128)(2,1)} %bitcast_bitcast_fusion) | copy-start | bytes 6291460
  98.0 13.3 %all-to-all-start.4 = ((f32[8,2,512]{2,1,0:T(2,128)}), f32[8,2,512]{2,1,0:T(2,128)S(1)}, u32[]{:S(2)}, u32[]{:S(2)}) async-start(f32[8,2,512]{2,1,0:T(2,128)} %reshape.340), calls=%async_computation.4 | async-start | bytes 65536 | tf_op jit(solution)/shard_map/all_to_all | solution.py:126
  111.2 16.1 %all-to-all-start.2 = ((f32[8,2,512]{2,1,0:T(2,128)}), f32[8,2,512]{2,1,0:T(2,128)S(1)}, u32[]{:S(2)}, u32[]{:S(2)}) async-start(f32[8,2,512]{2,1,0:T(2,128)} %reshape.331), calls=%async_computation.2 | async-start | bytes 65536 | tf_op jit(solution)/shard_map/all_to_all | solution.py:119
  127.4 48.9 %all-to-all-start.3 = ((bf16[8,2,512,128]{3,2,1,0:T(8,128)(2,1)}), bf16[8,2,512,128]{3,2,1,0:T(8,128)(2,1)S(1)}, u32[]{:S(2)}, u32[]{:S(2)}) async-start(bf16[8,2,512,128]{3,2,1,0:T(8,128)(2,1)} %bitcast.75), calls=%async_computation.3 | async-start | bytes 4194304 | tf_op jit(solution)/shard_map/all_to_all | solution.py:111
  132.8 125.6 %all-gather.2.cloned.1.call-start = ((), (), s32[]{:S(2)}) async-start(), calls=%async_computation.5 | async-start | bytes 10485760 | tf_op jit(solution)/shard_map/all_gather | solution.py:158
Sparse Core Ops, SparseCore 0:
  195.9 62.5 all-gather.1
where the time goes:
time: 282 us; the launch traced here: 280 us
  waiting for transfers between devices  107 us (38%)
  matrix products  58.3 us (21%)
  local copies, waits for them, and re-layouts  38.4 us (14%)
  other arithmetic  32.3 us (11%)
  starting transfers between devices  30.2 us (11%)
  between operations  13.6 us (5%)
    all_gather x1, waiting for transfers between devices, body(): lax.all_gather(attended, 'head', axis=1, tiled=True)  62.7 us
    all_to_all x1, waiting for transfers between devices, body(): lax.all_to_all(outgoing, 'seq', split_axis=0, concat_axis=0, tiled=True)  36.5 us
    dot_general x2, matrix products, tile_partial(): jnp.einsum('nqk,nkd->nqd', weights, value_tile, preferred_element_type=jn...  23 us
    dot_general x2, matrix products, tile_partial(): jnp.einsum('nqd,nkd->nqk', query_tile, key_tile, preferred_element_type=j...  20.7 us
    reduce_sum x2, other arithmetic, tile_partial(): totals = jnp.sum(shifted, axis=-1)  17.8 us
    dot_general x1, matrix products, body(): jnp.dot(lax.all_gather(attended, 'head', axis=1, tiled=True), out_weight,...  14.6 us
    reduce_sum x1, other arithmetic, body(): numer = jnp.sum(factor[..., None] * all_out.astype(jnp.float32), axis=1)  9.42 us
    all_to_all x1, starting transfers between devices, body(): lax.all_to_all(served_total.reshape(seq_count, capacity, block_rows), 'se...  8.29 us
  transfers between devices with their start and end apart: 6, of which 3 were waited for; matrix products, arithmetic and copies ran while one was open for 25% of the time, Pallas kernels for 0%

commit v1 on v0

v1 whole, which is shorter than its diff:
```python
import functools
import math

import jax
import jax.numpy as jnp
from jax import lax
from jax.experimental import pallas as pl
from jax.experimental.pallas import tpu as pltpu
from jax.sharding import PartitionSpec as P

CAP = 2
MESH = pl.DeviceIdType.MESH
F32 = jnp.float32
BF16 = jnp.bfloat16


def loop(lower, upper, step):
    def body(i, carry):
        step(i)
        return carry

    lax.fori_loop(lower, upper, body, 0)


def attend(query, key, value, causal_start=None):
    scale = query.shape[-1] ** -0.5
    scores = lax.dot_general(
        key, query, (((1,), (1,)), ((), ())), preferred_element_type=F32
    )
    if causal_start is not None:
        key_at = lax.broadcasted_iota(jnp.int32, scores.shape, 0)
        query_at = lax.broadcasted_iota(jnp.int32, scores.shape, 1) + causal_start
        scores = jnp.where(key_at <= query_at, scores, -jnp.inf)
    top = jnp.max(scores, axis=0, keepdims=True)
    weights = jnp.exp2((scores - top) * (scale * math.log2(math.e)))
    total = jnp.sum(weights, axis=0, keepdims=True)
    part = lax.dot_general(
        value, weights.astype(BF16), (((0,), (0,)), ((), ())), preferred_element_type=F32
    )
    return part / total, top * scale + jnp.log(total)


def plan_kernel(dims, picks, q, ask, slot, q_send, owner):
    n_seq, n_head, blocks, heads, n_pick, rows, width = dims
    pairs = blocks * heads
    me = lax.axis_index("seq")

    def find_owner(p):
        b, h = lax.div(p, heads), lax.rem(p, heads)
        found = [picks[b, h, t] for t in range(n_pick)]
        for t in range(n_pick):
            fresh = found[t] >= 0
            for earlier in range(t):
                fresh = fresh & (found[t] != found[earlier])
            owner[p * n_pick + t] = jnp.where(fresh, lax.div(found[t], blocks), -1)
            slot[p * n_pick + t] = -1

    loop(0, pairs, find_owner)

    def fill(s):
        def scan(p, carry):
            count, first, second = carry
            for t in range(n_pick):
                e = p * n_pick + t
                hit = owner[e] == s
                slot[e] = jnp.where(hit, s * CAP + count, slot[e])
                first = jnp.where(hit & (count == 0), e, first)
                second = jnp.where(hit & (count == 1), e, second)
                count = jnp.where(hit, count + 1, count)
            return count, first, second

        zero = jnp.int32(0)
        _, first, second = lax.fori_loop(0, pairs, scan, (zero, zero, zero))
        for c, e in enumerate((first, second)):
            p = lax.div(e, n_pick)
            pick = jnp.maximum(picks[lax.div(p, heads), lax.rem(p, heads), lax.rem(e, n_pick)], 0)
            ask[s, c] = lax.rem(pick, blocks) * heads + lax.rem(p, heads)
            q_send[s * CAP + c] = q[
                pl.ds(pl.multiple_of(lax.div(p, heads) * rows, rows), rows),
                pl.ds(pl.multiple_of(lax.rem(p, heads) * width, width), width),
            ]

    loop(0, me, fill)


def kernel(
    dims,
    q_hbm,
    k_hbm,
    v_hbm,
    ask,
    slot,
    q_send,
    w_hbm,
    out,
    q,
    k,
    v,
    w,
    asked,
    q_recv,
    o_send,
    o_recv,
    l_send,
    l_recv,
    own_o,
    own_l,
    gath,
    acc,
    load_sem,
    w_sem,
    ask_sem,
    qs_sem,
    os_sem,
    ls_sem,
    near_sem,
    cross_sem,
    fwd_sem,
):
    n_seq, n_head, blocks, heads, n_pick, rows, width = dims
    pairs = blocks * heads
    n_x = n_head // 2
    me = lax.axis_index("seq")
    hd = lax.axis_index("head")
    hx, hc = lax.div(hd, 2), lax.rem(hd, 2)
    mate = hx * 2 + 1 - hc

    def across(step):
        return lax.rem(hx + step, n_x) * 2 + hc

    def behind(step):
        return lax.rem(hx + n_x - step, n_x) * 2 + hc

    def load(i, p):
        src, dst = ((q_hbm, q), (k_hbm, k), (v_hbm, v))[i]
        b, h = lax.div(p, heads), lax.rem(p, heads)
        return pltpu.make_async_copy(
            src.at[
                pl.ds(pl.multiple_of(b * rows, rows), rows),
                pl.ds(pl.multiple_of(h * width, width), width),
            ],
            dst.at[p],
            load_sem.at[i, p],
        )

    def start_loads(p):
        for i in range(3):
            load(i, p).start()

    def end_loads(p):
        for i in range(3):
            load(i, p).wait()

    weight_load = pltpu.make_async_copy(w_hbm, w, w_sem.at[0])
    loop(0, pairs, start_loads)
    weight_load.start()

    barrier = pltpu.get_barrier_semaphore()

    def greet(d):
        pl.semaphore_signal(
            barrier, inc=1, device_id={"seq": lax.rem(me + d, n_seq)}, device_id_type=MESH
        )

    loop(1, n_seq, greet)
    for d in range(1, n_head):
        pl.semaphore_signal(
            barrier, inc=1, device_id={"head": lax.rem(hd + d, n_head)}, device_id_type=MESH
        )

    pl.semaphore_wait(barrier, n_seq + n_head - 2)

    def ask_copy(s, r):
        return pltpu.make_async_remote_copy(
            src_ref=ask.at[s],
            dst_ref=asked.at[r],
            send_sem=ask_sem.at[0, s],
            recv_sem=ask_sem.at[1, r],
            device_id={"seq": s},
            device_id_type=MESH,
        )

    def q_copy(s, r):
        return pltpu.make_async_remote_copy(
            src_ref=q_send.at[pl.ds(s * CAP, CAP)],
            dst_ref=q_recv.at[pl.ds(r * CAP, CAP)],
            send_sem=qs_sem.at[0, s],
            recv_sem=qs_sem.at[1, r],
            device_id={"seq": s},
            device_id_type=MESH,
        )

    def o_copy(r, s):
        return pltpu.make_async_remote_copy(
            src_ref=o_send.at[pl.ds(r * CAP, CAP)],
            dst_ref=o_recv.at[pl.ds(s * CAP, CAP)],
            send_sem=os_sem.at[0, r],
            recv_sem=os_sem.at[1, s],
            device_id={"seq": r},
            device_id_type=MESH,
        )

    def l_copy(r, s):
        return pltpu.make_async_remote_copy(
            src_ref=l_send.at[pl.ds(r * CAP, CAP)],
            dst_ref=l_recv.at[pl.ds(s * CAP, CAP)],
            send_sem=ls_sem.at[0, r],
            recv_sem=ls_sem.at[1, s],
            device_id={"seq": r},
            device_id_type=MESH,
        )

    def send_queries(s):
        ask_copy(s, me).start()
        q_copy(s, me).start()

    loop(0, me, send_queries)
    loop(0, pairs, end_loads)

    half = rows // 2

    def own(p):
        query, key, value = q[p], k[p], v[p]
        for part in range(2):
            seen = (part + 1) * half
            span = slice(part * half, seen)
            result, level = attend(query[span], key[:seen], value[:seen], part * half)
            own_o[p, :, span] = result
            own_l[p, :, span] = level

    def serve(r):
        ask_copy(me, r).wait_recv()
        q_copy(me, r).wait_recv()

        def one(c):
            code = asked[r, c]
            query, key, value = q_recv[r * CAP + c], k[code], v[code]
            for part in range(2):
                span = slice(part * half, (part + 1) * half)
                result, level = attend(query[span], key, value)
                o_send[r * CAP + c, :, span] = result.astype(BF16)
                l_send[r * CAP + c, :, span] = level

        loop(0, CAP, one)
        o_copy(r, me).start()
        l_copy(r, me).start()

    served = n_seq - 1 - me
    ahead = jnp.minimum(pairs, 4 * (me + 1))

    def round_of(t):
        lower = jnp.where(t == 0, 0, jnp.minimum(pairs, ahead + 2 * (t - 1)))
        upper = jnp.where(t == served, pairs, jnp.minimum(pairs, ahead + 2 * t))
        loop(lower, upper, own)

        @pl.when(t < served)
        def _():
            serve(n_seq - 1 - t)

    loop(0, served + 1, round_of)

    def collect(s):
        o_copy(s, s).wait_recv()
        l_copy(s, s).wait_recv()

    loop(0, me, collect)

    groups = heads // 2
    chunks = blocks * groups

    def head_copy(src, dst, sems, index, target):
        return pltpu.make_async_remote_copy(
            src_ref=gath.at[src, index],
            dst_ref=gath.at[dst, index],
            send_sem=sems[0],
            recv_sem=sems[1],
            device_id={"head": target},
            device_id_type=MESH,
        )

    def near_copy(index):
        return head_copy(hd, hd, (near_sem.at[0, index], near_sem.at[1, index]), index, mate)

    def cross_copy(step, index):
        sems = (cross_sem.at[0, step - 1, index], cross_sem.at[1, step - 1, index])
        return head_copy(hd, hd, sems, index, across(step))

    def fwd_copy(step, index):
        sems = (fwd_sem.at[0, step - 1, index], fwd_sem.at[1, step - 1, index])
        return head_copy(behind(step), behind(step), sems, index, mate)

    def merge(p):
        level = own_l[p]
        levels, slots = [], []
        for t in range(n_pick):
            at = slot[p * n_pick + t]
            safe = jnp.maximum(at, 0)
            far = l_recv[safe]
            levels.append(jnp.where(at >= 0, far, -jnp.inf))
            slots.append((at, safe))
        largest = level
        for far in levels:
            largest = jnp.maximum(largest, far)
        factor = jnp.exp(level - largest)
        denom = factor
        factors = []
        for far in levels:
            factors.append(jnp.exp(far - largest))
            denom = denom + factors[-1]
        numer = (factor / denom) * own_o[p]
        for (at, safe), far in zip(slots, factors):
            part = o_recv[safe].astype(F32)
            numer = numer + jnp.where(at >= 0, (far / denom) * part, 0.0)
        return numer.T.astype(BF16)

    def merge_group(index):
        for i in range(2):
            gath[hd, index, :, i * width : (i + 1) * width] = merge(index * 2 + i)
        for step in range(1, n_x):
            cross_copy(step, index).start()
        near_copy(index).start()

    loop(0, chunks, merge_group)
    weight_load.wait()

    depth = 2 * width

    def project(source, index, fresh=False):
        b, g = lax.div(index, groups), lax.rem(index, groups)
        at = pl.multiple_of((source * groups + g) * depth, depth)
        result = jnp.dot(
            gath[source, index], w[pl.ds(at, depth), :], preferred_element_type=F32
        )
        if fresh:
            acc[b] = result
        else:
            acc[b] += result

    def start_rows(b):
        acc[b] = jnp.zeros(acc.shape[1:], F32)

    loop(0, blocks, start_rows)
    loop(0, chunks, lambda index: project(hd, index))

    def take_near(index):
        near_copy(index).wait_recv()
        project(mate, index)

    loop(0, chunks, take_near)

    for step in range(1, n_x):

        def take_cross(index):
            cross_copy(step, index).wait_recv()
            fwd_copy(step, index).start()
            project(behind(step), index)
            fwd_copy(step, index).wait_recv()
            project(lax.rem(hx + n_x - step, n_x) * 2 + 1 - hc, index)

        loop(0, chunks, take_cross)

    def finish(b):
        out[pl.ds(pl.multiple_of(b * rows, rows), rows), :] = acc[b].astype(BF16)

    loop(0, blocks, finish)

    def sent_queries(s):
        ask_copy(s, me).wait_send()
        q_copy(s, me).wait_send()

    loop(0, me, sent_queries)

    def sent_results(r):
        o_copy(r, me).wait_send()
        l_copy(r, me).wait_send()

    loop(me + 1, n_seq, sent_results)

    def sent_heads(index):
        near_copy(index).wait_send()
        for step in range(1, n_x):
            cross_copy(step, index).wait_send()
            fwd_copy(step, index).wait_send()

    loop(0, chunks, sent_heads)


def solution(mesh):
    n_seq, n_head = mesh.shape["seq"], mesh.shape["head"]

    def body(query_rows, key_rows, value_rows, block_picks, out_weight):
        tok_rows, feature_width = query_rows.shape
        blocks, heads, n_pick = block_picks.shape
        rows, width = tok_rows // blocks, feature_width // heads
        pairs = blocks * heads
        chunks = pairs // 2
        n_x = n_head // 2
        any_spec = pl.BlockSpec(memory_space=pl.ANY)
        smem_spec = pl.BlockSpec(memory_space=pltpu.SMEM)
        vmem_spec = pl.BlockSpec(memory_space=pltpu.VMEM)
        out_width = out_weight.shape[1]
        slots = n_seq * CAP
        dma = pltpu.SemaphoreType.DMA
        dims = (n_seq, n_head, blocks, heads, n_pick, rows, width)
        ask, slot, q_send = pl.pallas_call(
            functools.partial(plan_kernel, dims),
            out_shape=(
                jax.ShapeDtypeStruct((n_seq, CAP), jnp.int32),
                jax.ShapeDtypeStruct((pairs * n_pick,), jnp.int32),
                jax.ShapeDtypeStruct((slots, rows, width), BF16),
            ),
            in_specs=[smem_spec, vmem_spec],
            out_specs=(smem_spec, smem_spec, vmem_spec),
            scratch_shapes=[pltpu.SMEM((pairs * n_pick,), jnp.int32)],
            name="plan",
        )(block_picks, query_rows)
        return pl.pallas_call(
            functools.partial(kernel, dims),
            out_shape=jax.ShapeDtypeStruct((tok_rows, out_width), BF16),
            in_specs=[any_spec] * 3 + [smem_spec] * 2 + [any_spec] * 2,
            out_specs=vmem_spec,
            scratch_shapes=[
                pltpu.VMEM((pairs, rows, width), BF16),
                pltpu.VMEM((pairs, rows, width), BF16),
                pltpu.VMEM((pairs, rows, width), BF16),
                pltpu.VMEM(out_weight.shape, BF16),
                pltpu.SMEM((n_seq, CAP), jnp.int32),
                pltpu.VMEM((slots, rows, width), BF16),
                pltpu.VMEM((slots, width, rows), BF16),
                pltpu.VMEM((slots, width, rows), BF16),
                pltpu.VMEM((slots, 1, rows), F32),
                pltpu.VMEM((slots, 1, rows), F32),
                pltpu.VMEM((pairs, width, rows), F32),
                pltpu.VMEM((pairs, 1, rows), F32),
                pltpu.VMEM((n_head, chunks, rows, 2 * width), BF16),
                pltpu.VMEM((blocks, rows, out_width), F32),
                dma((3, pairs)),
                dma((1,)),
                dma((2, n_seq)),
                dma((2, n_seq)),
                dma((2, n_seq)),
                dma((2, n_seq)),
                dma((2, chunks)),
                dma((2, max(n_x - 1, 1), chunks)),
                dma((2, max(n_x - 1, 1), chunks)),
            ],
            compiler_params=pltpu.CompilerParams(
                collective_id=0,
                has_side_effects=True,
                vmem_limit_bytes=67043328,
            ),
            name="layer",
        )(query_rows, key_rows, value_rows, ask, slot, q_send, out_weight)

    return jax.shard_map(
        body,
        mesh=mesh,
        in_specs=(
            P("seq", "head"),
            P("seq", "head"),
            P("seq", "head"),
            P("seq", "head", None),
            P(None, "head"),
        ),
        out_specs=P("seq", "head"),
        check_vma=False,
    )
```

time: 282 us -> 131 us (0.46)
  Pallas kernels: 0 us -> 126 us
  waiting for transfers between devices: 107 us -> 0 us
  matrix products: 58.3 us -> 0 us
  local copies, waits for them, and re-layouts: 38.4 us -> 4.43 us
  other arithmetic: 32.3 us -> 0 us
  starting transfers between devices: 30.2 us -> 0 us
  between operations: 13.6 us -> 0.02 us
    pallas_call x0 -> x2, Pallas kernels: none -> 126 us  [the longest x1 121 us: body(): pl.pallas_call(functools.partial(kernel, dims), out_shape=jax.ShapeDtypeS...]
    all_gather x1 -> x0, waiting for transfers between devices: 62.7 us -> none  [body(): lax.all_gather(attended, 'head', axis=1, tiled=True)]
    dot_general x5 -> x0, matrix products: 58.3 us -> none  [the longest x2 23 us: tile_partial(): jnp.einsum('nqk,nkd->nqd', weights, value_tile, preferred_element_type=jn...]
    all_to_all x5 -> x0, waiting for transfers between devices: 44.3 us -> none  [the longest x1 36.5 us: body(): lax.all_to_all(outgoing, 'seq', split_axis=0, concat_axis=0, tiled=True)]
    all_to_all x5 -> x0, starting transfers between devices: 30.2 us -> none  [the longest x1 8.29 us: body(): lax.all_to_all(served_total.reshape(seq_count, capacity, block_rows), 'se...]
    reduce_sum x5 -> x0, other arithmetic: 27.6 us -> none  [the longest x2 17.8 us: tile_partial(): totals = jnp.sum(shifted, axis=-1)]
    gather x6 -> x0, local copies, waits for them, and re-layouts: 17 us -> none  [the longest x1 5.74 us: body(): asking[sender].reshape(seq_count, capacity, block_rows, head_width)]
    transpose x7 -> x0, local copies, waits for them, and re-layouts: 5.55 us -> none  [the longest x6 4.19 us: by_head(): jnp.transpose(shaped, (0, 2, 1, 3))]
  transfers between devices with their start and end apart: 6 -> 0, of which waited for: 3 -> 0; matrix products, arithmetic and copies ran while one was open for 25% -> 0% of each run, Pallas kernels for 0% -> 0%
where the time goes in v1:
time: 131 us; the launch traced here: 130 us
  Pallas kernels  126 us (96%)
  local copies, waits for them, and re-layouts  4.43 us (3%)
    pallas_call x1, Pallas kernels, body(): pl.pallas_call(functools.partial(kernel, dims), out_shape=jax.ShapeDtypeS...  121 us
    pallas_call x1, Pallas kernels, body(): pl.pallas_call(functools.partial(plan_kernel, dims), out_shape=(jax.Shape...  5.08 us
    unnamed x2, local copies, waits for them, and re-layouts  4.43 us

profile of v1, /device:TPU:17, one launch (start us, length us, event | category | flops | bytes accessed | tf_op | source)
XLA Modules:
  0.0 130.4 jit_solution(12195770373680383626)
XLA Ops:
  0.0 1.4 %copy.6.picks = s32[2,8,4]{2,1,0:T(8,128)} copy(s32[2,8,4]{1,2,0:T(4,128)} %param.8) | data formatting | bytes 512 | tf_op args[3]
  1.4 5.1 %plan.1 = (s32[8,2]{1,0:T(8,128)}, s32[64]{0:T(128)}, bf16[16,512,128]{2,1,0:T(8,128)(2,1)}) custom-call(s32[2,8,4]{2,1,0:T(8,128)} %copy.6.picks, bf16[1024,1024]{1,0:T(8,128)(2,1)} %q_hbm.1), custom_call_target="tpu_custom_call" | custom-call | tf_op jit(solution)/shard_map/plan/pallas_call | solution.py:405
  6.4 120.9 %layer.1 = bf16[1024,1024]{1,0:T(8,128)(2,1)} custom-call(bf16[1024,1024]{1,0:T(8,128)(2,1)} %q_hbm.1, bf16[1024,1024]{1,0:T(8,128)(2,1)} %k_hbm.1, bf16[1024,1024]{1,0:T(8,128)(2,1)} %v_hbm.1, s32[8,2]{1,0:T(8,128)} %get-tuple-element.8.ask, s32[64]{0:T(128)} %get-tuple-element.9.slot, bf16[16,512,128]{2,1,0:T(8,128)(2,1)} %get-tuple-element.10.q_send, ...), custom_call_target="tpu_custom_call" | custom-call | tf_op jit(solution)/shard_map/layer/pallas_call | solution.py:417
  127.3 3.1 %copy.8 = bf16[1024,1024]{1,0:T(8,128)(2,1)} copy(bf16[1024,1024]{1,0:T(8,128)(2,1)} %layer.1) | data formatting | bytes 4194304

commit v2 on v1

--- a/solution.py
+++ b/solution.py
@@ -246,11 +246,11 @@
         l_copy(r, me).start()
 
     served = n_seq - 1 - me
-    ahead = jnp.minimum(pairs, 4 * (me + 1))
+    ahead = jnp.minimum(pairs, 2 * me + 4)
 
     def round_of(t):
-        lower = jnp.where(t == 0, 0, jnp.minimum(pairs, ahead + 2 * (t - 1)))
-        upper = jnp.where(t == served, pairs, jnp.minimum(pairs, ahead + 2 * t))
+        lower = jnp.where(t == 0, 0, jnp.minimum(pairs, ahead + t - 1))
+        upper = jnp.where(t == served, pairs, jnp.minimum(pairs, ahead + t))
         loop(lower, upper, own)
 
         @pl.when(t < served)

time: 131 us -> 131 us (level)
  no operation moved by 1% of the time
where the time goes in v2:
time: 131 us; the launch traced here: 130 us
  Pallas kernels  126 us (96%)
  local copies, waits for them, and re-layouts  4.43 us (3%)
    pallas_call x1, Pallas kernels, body(): pl.pallas_call(functools.partial(kernel, dims), out_shape=jax.ShapeDtypeS...  121 us
    pallas_call x1, Pallas kernels, body(): pl.pallas_call(functools.partial(plan_kernel, dims), out_shape=(jax.Shape...  5.08 us
    unnamed x2, local copies, waits for them, and re-layouts  4.43 us

profile of v2, /device:TPU:17, one launch (start us, length us, event | category | flops | bytes accessed | tf_op | source)
XLA Modules:
  0.0 130.4 jit_solution(15760731502974960468)
XLA Ops:
  0.0 1.4 %copy.6.picks = s32[2,8,4]{2,1,0:T(8,128)} copy(s32[2,8,4]{1,2,0:T(4,128)} %param.8) | data formatting | bytes 512 | tf_op args[3]
  1.4 5.1 %plan.1 = (s32[8,2]{1,0:T(8,128)}, s32[64]{0:T(128)}, bf16[16,512,128]{2,1,0:T(8,128)(2,1)}) custom-call(s32[2,8,4]{2,1,0:T(8,128)} %copy.6.picks, bf16[1024,1024]{1,0:T(8,128)(2,1)} %q_hbm.1), custom_call_target="tpu_custom_call" | custom-call | tf_op jit(solution)/shard_map/plan/pallas_call | solution.py:405
  6.4 120.9 %layer.1 = bf16[1024,1024]{1,0:T(8,128)(2,1)} custom-call(bf16[1024,1024]{1,0:T(8,128)(2,1)} %q_hbm.1, bf16[1024,1024]{1,0:T(8,128)(2,1)} %k_hbm.1, bf16[1024,1024]{1,0:T(8,128)(2,1)} %v_hbm.1, s32[8,2]{1,0:T(8,128)} %get-tuple-element.8.ask, s32[64]{0:T(128)} %get-tuple-element.9.slot, bf16[16,512,128]{2,1,0:T(8,128)(2,1)} %get-tuple-element.10.q_send, ...), custom_call_target="tpu_custom_call" | custom-call | tf_op jit(solution)/shard_map/layer/pallas_call | solution.py:417
  127.3 3.1 %copy.8 = bf16[1024,1024]{1,0:T(8,128)(2,1)} copy(bf16[1024,1024]{1,0:T(8,128)(2,1)} %layer.1) | data formatting | bytes 4194304
